TPU v7x, 32 devices: a whole 2x2x4 slice. The times are simulated.
32 devices in a mesh: row: 4 (over z), col: 8 (over y, x, core).
Axes of the slice: x: 2, y: 2, z: 4, core: 2. Of those that a mesh axis runs over, the one named last changes fastest.
Arguments:
- train_points: float32 [4, 32, 4096], P('row', None, 'col'), as said below
- targets: float32 [4, 4096], P('row', 'col'), may hold values from -16 to 16
- inverse_factor: float32 [4, 4096, 1024], P('row', 'col')
- counts: int32 [4, 4], P('row'), may hold values from 512 to 1024, as said below
- membership: int32 [4, 4, 16], replicated, may hold values from 0 to 1, as said below
- test_points: float32 [16, 32, 128], P('row'), may hold values from -6 to 6
Outputs:
- pred_mean: float32 [16, 128], P('row')
- pred_var: float32 [16, 128], P('row')
Inputs may be any that keep to these rules, and one draw needn't show every extreme that they name: Each expert membership[r, c, :] takes part in at least one and at most 4 blocks, exactly 4 for at least one expert, and in at most one of the 4 blocks of each owner row. `counts`: at least one expert has all 1024 points valid. `train_points`: each expert's 1024 points are drawn independently of the other experts' points.
All inputs are finite; a program needn't handle non-finite values.
Results may differ from a plain program's by a relative error of at most 0.0003.
Values sent between devices are 32-bit elements; how exact they have to be, the bound alone decides.
A program may use at most 64 MiB of HBM per device.

v0:
```python
import jax
import jax.numpy as jnp
from jax import lax
from jax.sharding import PartitionSpec as P

SIGNAL = 1.0
NOISE = 0.1
HIGHEST = lax.Precision.HIGHEST


def partner_2(block, axis, distance):
    count = lax.axis_size(axis)
    route = []
    for low in range(count):
        high = low | 1 << distance
        if high != low and high < count:
            route += [(low, high), (high, low)]
    return lax.ppermute(block, axis, route)


def cross_kernel(train_cols, test_cols, squared_scale):
    products = jnp.einsum("dn,dp->np", train_cols, test_cols, precision=HIGHEST)
    spread = (
        jnp.sum(train_cols * train_cols, axis=0)[:, None]
        + jnp.sum(test_cols * test_cols, axis=0)[None, :]
        - 2.0 * products
    )
    return SIGNAL * jnp.exp(-0.5 * spread / squared_scale)


def slot_table(member, slot_count):
    before = jnp.cumsum(member) - member
    slot_ids = jnp.arange(slot_count, dtype=jnp.int32)[:, None]
    picked = ((member[None, :] == 1) & (before[None, :] == slot_ids)).astype(jnp.int32)
    chosen = jnp.sum(picked * jnp.arange(member.shape[0], dtype=jnp.int32)[None, :], axis=1)
    return (picked.astype(jnp.float32), chosen)


def weigh_expert(mean_part, quad_part):
    variance = NOISE + jnp.maximum(SIGNAL - quad_part, 0.0)
    entropy_gap = 0.5 * (jnp.log(SIGNAL + NOISE) - jnp.log(variance))
    weight = entropy_gap / variance
    return (weight * mean_part, weight)


def on_device(train_points, targets, inverse_factor, counts, membership, test_points):
    parity = lax.axis_index("col") % 2
    expert_col = lax.axis_index("col") // 2
    own_row = lax.axis_index("row")
    row_count = lax.axis_size("row")
    slot_count = min(8, row_count)
    features = train_points.shape[1]
    rows_half = train_points.shape[2]
    blocks_own = test_points.shape[0]
    block_len = test_points.shape[2]
    squared_scale = 0.5 * features
    own_points = train_points[0]
    own_targets = targets[0]
    packed = jnp.concatenate([own_points, own_targets[None, :]], axis=0)
    partner = partner_2(packed, "col", 0)
    other_points = partner[:features]
    other_targets = partner[features]
    member = membership[own_row, expert_col]
    picked, chosen = slot_table(member, slot_count)
    wanted = lax.dynamic_slice_in_dim(
        membership[:, expert_col], own_row * blocks_own, blocks_own, 1
    )
    gathered = lax.all_gather(test_points, "row", axis=0, tiled=True)
    slot_tests = gathered[chosen]
    test_cols = slot_tests.transpose(1, 0, 2).reshape(features, slot_count * block_len)
    valid_count = counts[0, expert_col]
    local_index = jnp.arange(rows_half, dtype=jnp.int32)
    own_valid = 2 * local_index + parity < valid_count
    other_valid = 2 * local_index + (1 - parity) < valid_count
    own_kernel = jnp.where(
        own_valid[:, None], cross_kernel(own_points, test_cols, squared_scale), 0.0
    )
    other_kernel = jnp.where(
        other_valid[:, None], cross_kernel(other_points, test_cols, squared_scale), 0.0
    )
    factor_pairs = inverse_factor[0].reshape(rows_half, rows_half, 2)
    own_part = lax.dynamic_index_in_dim(factor_pairs, parity, 2, keepdims=False)
    other_part = lax.dynamic_index_in_dim(factor_pairs, 1 - parity, 2, keepdims=False)
    solved = jnp.dot(own_part, own_kernel, precision=HIGHEST, preferred_element_type=jnp.float32)
    solved = solved + jnp.dot(
        other_part, other_kernel, precision=HIGHEST, preferred_element_type=jnp.float32
    )
    whitened = jnp.dot(own_part, own_targets, precision=HIGHEST, preferred_element_type=jnp.float32)
    whitened = whitened + jnp.dot(
        other_part, other_targets, precision=HIGHEST, preferred_element_type=jnp.float32
    )
    mean_own = jnp.dot(whitened, solved, precision=HIGHEST, preferred_element_type=jnp.float32)
    quad_own = jnp.sum(solved * solved, axis=0)
    partials = partner_2(jnp.stack([mean_own, quad_own], axis=0), "col", 0)
    weighted, weight = weigh_expert(mean_own + partials[0], quad_own + partials[1])
    slot_ids = jnp.arange(slot_count, dtype=jnp.int32)
    my_slots = (slot_ids % 2 == parity).astype(jnp.float32)[:, None]
    my_picked = picked * my_slots
    dense_num = jnp.einsum(
        "sb,sp->bp", my_picked, weighted.reshape(slot_count, block_len), precision=HIGHEST
    )
    dense_wgt = jnp.einsum(
        "sb,sp->bp", my_picked, weight.reshape(slot_count, block_len), precision=HIGHEST
    )
    row_num = jnp.sum(dense_num.reshape(row_count, blocks_own, block_len), axis=1)
    row_wgt = jnp.sum(dense_wgt.reshape(row_count, blocks_own, block_len), axis=1)
    outgoing_sums = jnp.stack([row_num, row_wgt], axis=1)
    arrived = lax.all_to_all(outgoing_sums, "row", split_axis=0, concat_axis=0, tiled=True)
    placed = jnp.einsum("rj,rkp->kjp", wanted.astype(jnp.float32), arrived, precision=HIGHEST)
    total_num, total_wgt = lax.psum((placed[0], placed[1]), "col")
    precision_sum = 1.0 / (SIGNAL + NOISE) + total_wgt
    return (total_num / precision_sum, 1.0 / precision_sum)


def solution(mesh):
    in_specs = (
        P("row", None, "col"),
        P("row", "col"),
        P("row", "col", None),
        P("row", None),
        P(),
        P("row", None, None),
    )
    out_specs = (P("row", None), P("row", None))
    return jax.shard_map(
        on_device, mesh=mesh, in_specs=in_specs, out_specs=out_specs, check_vma=False
    )
```

profile of v0, /device:TPU:0, one launch (start us, length us, event | category | flops | bytes accessed | tf_op | source)
XLA Modules:
  0.0 70.3 jit_solution(5931016102477284509)
XLA Ops:
  0.6 0.9 %pad_maximum_fusion = f32[33,512]{1,0:T(8,128)S(1)} fusion(f32[1,512]{1,0:T(1,128)} %param.7, f32[32,512]{1,0:T(8,128)} %bitcast.99), kind=kLoop, calls=%fused_computation.30 | loop fusion | flops 16896 | bytes 135168 | tf_op jit(solution)/shard_map/concatenate | solution.py:59
  1.5 0.5 collective-permute-start
  2.0 0.9 %multiply_reduce_fusion.2 = f32[512]{0:T(512)S(1)} fusion(f32[1,32,512]{2,1,0:T(8,128)} %param.6), kind=kLoop, calls=%fused_computation.36 | loop fusion | flops 32256 | bytes 67584 | tf_op jit(solution)/shard_map/reduce_sum | solution.py:24
  2.9 3.0 %copy.30 = f32[1,512,1024]{1,2,0:T(8,128)} copy(f32[1,512,1024]{2,1,0:T(8,128)} %param.8) | data formatting | bytes 4194304 | tf_op args[2]
  5.8 2.5 %reshape_squeeze.3 = f32[512,512,2]{0,2,1:T(2,128)S(1)} reshape(f32[1,512,1024]{1,2,0:T(8,128)} %copy.30) | data formatting | bytes 4194304 | tf_op jit(solution)/shard_map/reshape;squeeze | solution.py:81
  8.3 2.8 %constant_dynamic-slice_fusion = (f32[512,512,1]{0,2,1:T(1,128)}, f32[512,512,1]{0,2,1:T(1,128)S(1)}) fusion(f32[512,512,2]{0,2,1:T(2,128)S(1)} %reshape_squeeze.3, s32[]{:T(128)S(6)} %select_n.68, s32[]{:T(128)S(6)} %select_n.65), kind=kLoop, calls=%fused_computation.76 | loop fusion | bytes 4194312 | tf_op jit(solution)/shard_map/jit(dynamic_index_in_dim)/dynamic_slice | solution.py:83
  11.1 2.4 %copy.34 = f32[512,512,1]{1,0,2:T(8,128)S(1)} copy(f32[512,512,1]{0,2,1:T(1,128)} %get-tuple-element.6) | data formatting | bytes 2097152 | tf_op jit(solution)/shard_map/jit(dynamic_index_in_dim)/dynamic_slice | solution.py:83
  13.5 1.3 %copy.31 = f32[512,512,1]{1,0,2:T(8,128)S(1)} copy(f32[512,512,1]{0,2,1:T(1,128)S(1)} %get-tuple-element.7) | data formatting | bytes 2097152 | tf_op jit(solution)/shard_map/jit(dynamic_index_in_dim)/dynamic_slice | solution.py:82
  14.8 1.0 %fusion.8 = f32[1,512]{1,0:T(1,128)S(1)} fusion(f32[512,512,1]{1,0,2:T(8,128)S(1)} %copy.31, f32[1,512]{1,0:T(1,128)S(1)} %copy-done.3), kind=kOutput, calls=%fused_computation.15 | convolution fusion | flops 3145728 | bytes 1052672 | tf_op jit(solution)/shard_map/dot_general | solution.py:88
  15.8 0.7 %bitcast_compare_fusion = (pred[16]{0:T(512)(128)(4,1)S(1)}, s32[1,1,16]{2,1,0:T(1,128)S(1)}) fusion(s32[4,4,16]{2,1,0:T(4,128)} %param.10, s32[]{:T(128)S(6)} %select_n.60, s32[]{:T(128)S(6)} %select_n.62), kind=kLoop, calls=%fused_computation.83 | loop fusion | flops 16 | bytes 152 | tf_op jit(solution)/shard_map/eq | solution.py:34
  16.9 15.2 %all_gather.3 = f32[16,32,128]{2,1,0:T(8,128)S(1)} all-gather(f32[4,32,128]{2,1,0:T(8,128)S(1)} %copy-done.2), channel_id=1, replica_groups=mesh['row'=4,'col'=8] {'row'}, dimensions={0}, use_global_device_ids=true | all-gather | bytes 327680 | tf_op jit(solution)/shard_map/all_gather | solution.py:68
  32.2 0.6 gather_fusion
  32.8 0.6 constant_dynamic-slice_fusion.1
  33.4 0.7 add_compare_fusion.1
  34.0 1.2 %fusion.4 = f32[512,512]{0,1:T(8,128)S(1)} fusion(f32[512]{0:T(512)S(1)} %bitcast.101, f32[512]{0:T(512)S(1)} %multiply_reduce_fusion.2, pred[512]{0:T(512)(128)(4,1)S(1)} %add_compare_fusion.1, f32[1,32,512]{2,1,0:T(8,128)S(1)} %copy-done.1, f32[4,32,128]{2,1,0:T(8,128)S(1)} %gather_fusion), kind=kOutput, calls=%fused_computation.8 | convolution fusion | flops 101974016 | bytes 1184256 | tf_op jit(solution)/shard_map/dn,dp->np/dot_general | solution.py:22
  35.2 1.9 %fusion.10 = f32[512,512]{1,0:T(8,128)S(1)} fusion(f32[512,512]{0,1:T(8,128)S(1)} %fusion.4, f32[512,512,1]{1,0,2:T(8,128)S(1)} %copy.31), kind=kOutput, calls=%fused_computation.17 | convolution fusion | flops 1610612736 | bytes 3145728 | tf_op jit(solution)/shard_map/dot_general | solution.py:84
  37.1 0.5 broadcast.207
  37.6 0.7 reduce.6
  38.4 0.7 add_compare_fusion
  39.1 1.0 %fusion.5 = f32[1,512]{1,0:T(1,128)S(1)} fusion(f32[512,512,1]{1,0,2:T(8,128)S(1)} %copy.34, f32[33,512]{1,0:T(8,128)S(1)} %collective-permute-done), kind=kOutput, calls=%fused_computation.12 | convolution fusion | flops 3145728 | bytes 1052672 | tf_op jit(solution)/shard_map/dot_general | solution.py:89
  40.1 1.0 %convolution_multiply_fusion = f32[512,512]{0,1:T(8,128)S(1)} fusion(f32[33,512]{1,0:T(8,128)S(1)} %collective-permute-done, f32[4,32,128]{2,1,0:T(8,128)S(1)} %gather_fusion), kind=kOutput, calls=%fused_computation.2 | convolution fusion | flops 100925440 | bytes 1179648 | tf_op jit(solution)/shard_map/dn,dp->np/dot_general | solution.py:22
  41.1 2.1 %multiply_reduce_fusion = (f32[512]{0:T(512)S(1)}, f32[512,512]{1,0:T(8,128)S(1)}) fusion(f32[512,512]{1,0:T(8,128)S(1)} %fusion.10, f32[512,512]{0,1:T(8,128)S(1)} %convolution_multiply_fusion, f32[512]{0:T(512)S(1)} %multiply_reduce_fusion.1, f32[512]{0:T(512)S(1)} %bitcast.102, pred[512]{0:T(512)(128)(4,1)S(1)} %add_compare_fusion, ...), kind=kOutput, calls=%fused_computation.19 | convolution fusion | flops 1612447232 | bytes 4200960 | tf_op jit(solution)/shard_map/dot_general | solution.py:85
  43.3 0.6 fusion.51
  44.1 1.1 %collective-permute-done.1 = f32[2,512]{1,0:T(2,128)S(1)} collective-permute-done((f32[2,512]{1,0:T(2,128)S(1)}, f32[2,512]{1,0:T(2,128)S(1)}, u32[]{:S(2)}, u32[]{:S(2)}) %collective-permute-start.1) | collective-permute-done | bytes 4128 | tf_op jit(solution)/shard_map/ppermute | solution.py:18
  45.1 0.3 convolution_reduce_fusion
  45.4 0.3 convolution_reduce_fusion.1
  45.6 0.6 pad_maximum_fusion.2
  46.3 5.2 %all-to-all-start = ((f32[4,2,128]{2,1,0:T(2,128)}), f32[4,2,128]{2,1,0:T(2,128)S(1)}, u32[]{:S(2)}, u32[]{:S(2)}) async-start(f32[4,2,128]{2,1,0:T(2,128)} %pad_maximum_fusion.2), calls=%async_computation | async-start | bytes 8192 | tf_op jit(solution)/shard_map/all_to_all | solution.py:108
  51.4 0.8 %dynamic-slice_convert_fusion = f32[4,1,4]{2,1,0:T(1,128)S(1)} fusion(s32[4,4,16]{2,1,0:T(4,128)} %param.10, s32[]{:T(128)S(6)} %select_n.70, s32[]{:T(128)S(6)} %select_n.72), kind=kLoop, calls=%fused_computation.62 | loop fusion | flops 16 | bytes 136 | tf_op jit(solution)/shard_map/convert_element_type | solution.py:109
  52.2 4.8 %all-to-all-done = f32[4,2,128]{2,1,0:T(2,128)S(1)} async-done(((f32[4,2,128]{2,1,0:T(2,128)}), f32[4,2,128]{2,1,0:T(2,128)S(1)}, u32[]{:S(2)}, u32[]{:S(2)}) %all-to-all-start) | async-done | bytes 4128 | tf_op jit(solution)/shard_map/all_to_all | solution.py:108
  57.2 12.6 %all-reduce = (f32[4,128]{1,0:T(4,128)S(1)}, f32[4,128]{1,0:T(4,128)S(1)}) all-reduce(f32[4,128]{1,0:T(4,128)S(1)} %get-tuple-element.9, f32[4,128]{1,0:T(4,128)S(1)} %get-tuple-element.8), channel_id=1, replica_groups=mesh['row'=4,'col'=8] {'col'}, use_global_device_ids=true, to_apply=%region_8.9 | all-reduce | flops 1024 | bytes 8192 | tf_op jit(solution)/shard_map/psum | solution.py:110
  69.7 0.6 add_divide_fusion
  (29 shorter events, 0.9 us)
Async XLA Ops:
  0.6 32.1 %copy-start = (s32[1,4]{1,0:T(1,128)S(1)}, s32[1,4]{1,0:T(1,128)}, u32[]{:S(2)}) copy-start(s32[1,4]{1,0:T(1,128)} %param.9) | copy-start | bytes 52
  1.5 37.5 %collective-permute-start = (f32[33,512]{1,0:T(8,128)S(1)}, f32[33,512]{1,0:T(8,128)S(1)}, u32[]{:S(2)}, u32[]{:S(2)}) collective-permute-start(f32[33,512]{1,0:T(8,128)S(1)} %pad_maximum_fusion), channel_id=1, source_target_pairs={{0,1},{1,0},{2,3},{3,2},{4,5},{5,4},{6,7},{7,6},{8,9},{9,8},{10,11... | collective-permute-start | bytes 202760 | tf_op jit(solution)/shard_map/ppermute | solution.py:18
  11.1 3.7 %copy-start.3 = (f32[1,512]{1,0:T(1,128)S(1)}, f32[1,512]{1,0:T(1,128)}, u32[]{:S(2)}) copy-start(f32[1,512]{1,0:T(1,128)} %param.7) | copy-start | bytes 6148
  13.5 3.4 %copy-start.2 = (f32[4,32,128]{2,1,0:T(8,128)S(1)}, f32[4,32,128]{2,1,0:T(8,128)}, u32[]{:S(2)}) copy-start(f32[4,32,128]{2,1,0:T(8,128)} %param.11) | copy-start | bytes 196612
  13.5 20.5 %copy-start.1 = (f32[1,32,512]{2,1,0:T(8,128)S(1)}, f32[1,32,512]{2,1,0:T(8,128)}, u32[]{:S(2)}) copy-start(f32[1,32,512]{2,1,0:T(8,128)} %param.6) | copy-start | bytes 196612
  43.9 1.2 %collective-permute-start.1 = (f32[2,512]{1,0:T(2,128)S(1)}, f32[2,512]{1,0:T(2,128)S(1)}, u32[]{:S(2)}, u32[]{:S(2)}) collective-permute-start(f32[2,512]{1,0:T(2,128)S(1)} %pad_maximum_fusion.1), channel_id=1, source_target_pairs={{0,1},{1,0},{2,3},{3,2},{4,5},{5,4},{6,7},{7,6},{8,9},{9,8},{10,11... | collective-permute-start | bytes 12296 | tf_op jit(solution)/shard_map/ppermute | solution.py:18
  46.3 10.7 %all-to-all-start = ((f32[4,2,128]{2,1,0:T(2,128)}), f32[4,2,128]{2,1,0:T(2,128)S(1)}, u32[]{:S(2)}, u32[]{:S(2)}) async-start(f32[4,2,128]{2,1,0:T(2,128)} %pad_maximum_fusion.2), calls=%async_computation | async-start | bytes 8192 | tf_op jit(solution)/shard_map/all_to_all | solution.py:108
where the time goes:
time: 70.8 us; the launch traced here: 70.3 us
  blocking collectives  27.8 us (39%)
  local copies, waits for them, and re-layouts  13.8 us (19%)
  matrix products  9.53 us (13%)
  other arithmetic  6.76 us (10%)
  waiting for transfers between devices  5.86 us (8%)
  starting transfers between devices  5.72 us (8%)
  between operations  0.83 us (1%)
    all_gather x1, blocking collectives, on_device(): gathered = lax.all_gather(test_points, 'row', axis=0, tiled=True)  15.2 us
    psum x1, blocking collectives, on_device(): total_num, total_wgt = lax.psum((placed[0], placed[1]), 'col')  12.6 us
    all_to_all x1, starting transfers between devices, on_device(): lax.all_to_all(outgoing_sums, 'row', split_axis=0, concat_axis=0, tiled=T...  5.16 us
    dynamic_slice x2, local copies, waits for them, and re-layouts, on_device(): lax.dynamic_index_in_dim(factor_pairs, 1 - parity, 2, keepdims=False)  5.15 us
    all_to_all x1, waiting for transfers between devices, on_device(): lax.all_to_all(outgoing_sums, 'row', split_axis=0, concat_axis=0, tiled=T...  4.81 us
    unnamed x9, local copies, waits for them, and re-layouts  2.98 us
    another operation x1, local copies, waits for them, and re-layouts, on_device(): factor_pairs = inverse_factor[0].reshape(rows_half, rows_half, 2)  2.49 us
    dot_general x2, matrix products, cross_kernel(): products = jnp.einsum('dn,dp->np', train_cols, test_cols, precision=HIGHEST)  2.25 us
  transfers between devices with their start and end apart: 3, of which 2 were waited for; matrix products, arithmetic and copies ran while one was open for 32% of the time, Pallas kernels for 0%

commit v1 on v0

v1 whole, which is shorter than its diff:
```python
import functools

import jax
import jax.numpy as jnp
from jax import lax
from jax.experimental import pallas as pl
from jax.experimental.pallas import tpu as pltpu
from jax.sharding import PartitionSpec as P

SIGNAL = 1.0
NOISE = 0.1
F32 = jnp.float32
BF16 = jnp.bfloat16
MESH = pl.DeviceIdType.MESH


def high_low(value):
    high = value.astype(BF16)
    return high, (value - high.astype(F32)).astype(BF16)


def expert_kernel(
    rows, cols,
    counts_hbm, member_hbm, train_ref, target_ref, factor_ref, test_ref,
    sums_ref,
    factor_buf, own_x, own_y, tests, other_x, other_y, sent_tests, got_tests,
    factor_high, factor_low, nat_a, nat_b, points, k_high, k_low,
    sent_parts, got_parts, taken_by, sent_bytes, alpha, counts_ref, member_ref,
    local_sems, x_send, x_recv, t_send, t_recv, p_send, p_recv,
):
    row = lax.axis_index("row")
    col = lax.axis_index("col")
    parity = col % 2
    expert = col // 2
    experts = cols // 2
    blocks, features, length = tests.shape
    half = own_x.shape[1]
    partner = (row, expert * 2 + 1 - parity)

    others = [lax.rem(row + d, rows) for d in range(1, rows)]
    mates = [lax.rem(expert + d, experts) for d in range(1, experts)]
    barrier = pltpu.get_barrier_semaphore()
    peers = [partner]
    for r in others:
        peers += [(r, expert * 2), (r, expert * 2 + 1)]
    for c in mates:
        peers += [(row, c * 2), (row, c * 2 + 1)]
    for peer in peers:
        pl.semaphore_signal(barrier, inc=1, device_id=peer, device_id_type=MESH)

    load_member = pltpu.make_async_copy(member_hbm, member_ref, local_sems.at[4])
    load_counts = pltpu.make_async_copy(counts_hbm, counts_ref, local_sems.at[5])
    load_tests = pltpu.make_async_copy(test_ref, tests, local_sems.at[0])
    load_member.start()
    load_x = pltpu.make_async_copy(train_ref.at[0], own_x, local_sems.at[1])
    load_y = pltpu.make_async_copy(target_ref, own_y, local_sems.at[2])
    load_f = pltpu.make_async_copy(factor_ref.at[0], factor_buf, local_sems.at[3])
    load_tests.start()
    load_x.start()
    load_y.start()
    load_counts.start()
    load_f.start()

    def chosen_in(row_at, owner):
        at = jnp.int32(0)
        for j in range(1, blocks):
            at = at + j * member_ref[row_at, expert, owner * blocks + j]
        return at

    load_member.wait()
    load_tests.wait()
    for d, r in enumerate(others):
        sent_tests[d] = tests[chosen_in(r, row)]
    pl.semaphore_wait(barrier, len(peers))

    def remote(src, dst, send, recv, peer):
        copy = pltpu.make_async_remote_copy(
            src_ref=src, dst_ref=dst, send_sem=send, recv_sem=recv,
            device_id=peer, device_id_type=MESH,
        )
        copy.start()
        return copy

    load_x.wait()
    load_y.wait()
    x_copy = remote(own_x, other_x, x_send.at[0], x_recv.at[0], partner)
    y_copy = remote(own_y, other_y, x_send.at[1], x_recv.at[1], partner)
    test_copies = [
        remote(sent_tests.at[d], got_tests.at[d], t_send.at[d], t_recv.at[d],
               (r, col))
        for d, r in enumerate(others)
    ]

    def stacked(x, y):
        xh = x.astype(BF16).astype(F32)
        xl = x - xh
        x2 = jnp.sum(x * x, axis=0, keepdims=True)
        a = x2.astype(BF16).astype(F32)
        b = (x2 - a).astype(BF16).astype(F32)
        c = x2 - a - b
        yh = y.astype(BF16).astype(F32)
        yl = y - yh
        at = lax.broadcasted_iota(jnp.int32, (8, half), 0)
        tail = jnp.zeros((8, half), F32)
        for i, v in enumerate((a, b, c, yh, yl)):
            tail = jnp.where(at == i, v, tail)
        first = jnp.concatenate([xh, xl, xh, xl], axis=0)
        last = jnp.concatenate([tail, jnp.zeros((120, half), F32)], axis=0)
        return first.T, last.T

    def put(a, b, offset):
        nat_a[pl.ds(offset, half, stride=2), :] = a
        nat_b[pl.ds(offset, half, stride=2), :] = b

    a, b = stacked(own_x[...], own_y[...])

    @pl.when(parity == 0)
    def _():
        put(a, b, 0)

    @pl.when(parity == 1)
    def _():
        put(a, b, 1)

    load_f.wait()
    fh, fl = high_low(factor_buf[...])
    factor_high[...] = fh
    factor_low[...] = fl

    x_copy.wait_recv()
    y_copy.wait_recv()
    a2, b2 = stacked(other_x[...], other_y[...])

    @pl.when(parity == 1)
    def _():
        put(a2, b2, 0)

    @pl.when(parity == 0)
    def _():
        put(a2, b2, 1)

    points[:, :128] = nat_a[...].astype(BF16)
    points[:, 128:] = nat_b[...].astype(BF16)
    solved_y = jnp.dot(factor_high[...], points[:, 128:], preferred_element_type=F32)
    solved_y += jnp.dot(factor_low[...], points[:, 128:], preferred_element_type=F32)
    whitened = solved_y[:, 3:4] + solved_y[:, 4:5]
    solved_back = jnp.sum(factor_buf[...] * whitened, axis=0, keepdims=True)
    for i in range(0, 2 * half, 128):
        alpha[i:i + 128, :] = jnp.broadcast_to(solved_back[:, i:i + 128], (128, 128)).T

    load_counts.wait()
    valid = counts_ref[0, expert]
    pair = 2 * length
    tail_at = lax.broadcasted_iota(jnp.int32, (128, pair), 0)
    tail_t = jnp.where(tail_at < 3, -1.0, 0.0).astype(BF16)
    chunk = 128
    order = [None] + list(range(rows - 1))
    owners = [row] + [lax.rem(row + rows - d - 1, rows) for d in range(rows - 1)]
    for first in range(0, rows, 2):
        taken = []
        for s in (first, first + 1):
            d = order[s]
            if d is None:
                taken.append(tests[chosen_in(row, row)])
            else:
                test_copies[d].wait_recv()
                taken.append(got_tests[d])
        t = jnp.concatenate(taken, axis=1)
        th, tl = high_low(2.0 * t)
        t2 = jnp.sum(t * t, axis=0, keepdims=True)
        rhs = jnp.concatenate([th, th, tl, tl, tail_t], axis=0)
        mean = jnp.zeros((1, pair), F32)
        for i in range(0, 2 * half, chunk):
            e = jnp.dot(points[i:i + chunk, :], rhs, preferred_element_type=F32) - t2
            k = jnp.exp(e * (1.0 / features))
            at = lax.broadcasted_iota(jnp.int32, (chunk, pair), 0) + i
            k = jnp.where(at < valid, SIGNAL * k, 0.0)
            along = alpha[i:i + chunk, :]
            mean += jnp.sum(k * jnp.concatenate([along, along], axis=1), axis=0, keepdims=True)
            kh, kl = high_low(k)
            k_high[i:i + chunk, :] = kh
            k_low[i:i + chunk, :] = kl
        solved = jnp.dot(factor_high[...], k_high[...], preferred_element_type=F32)
        solved += jnp.dot(factor_low[...], k_high[...], preferred_element_type=F32)
        solved += jnp.dot(factor_high[...], k_low[...], preferred_element_type=F32)
        quad = jnp.sum(solved * solved, axis=0, keepdims=True)
        for n, s in enumerate((first, first + 1)):
            lanes = slice(n * length, (n + 1) * length)
            d = order[s]
            sent_parts[s, 0:1, :] = mean[:, lanes]
            sent_parts[s, 1:2, :] = quad[:, lanes]
            mine = got_parts.at[expert, parity, row]
            if d is None:
                keep = pltpu.make_async_copy(sent_parts.at[s], mine, p_recv.at[0])
                keep.start()
                targets = [partner]
                for c in mates:
                    targets += [(row, c * 2), (row, c * 2 + 1)]
            else:
                targets = [(owners[s], lax.rem(col + c, cols)) for c in range(cols)]
            for target in targets:
                remote(sent_parts.at[s], mine, p_send.at[s], p_recv.at[0], target)

    for j in range(blocks):
        for e in range(experts):
            for r in range(rows):
                on = member_ref[r, e, row * blocks + j]
                n = e * rows + r
                taken_by[j, n:n + 1, :] = jnp.full((1, length), on, jnp.int32).astype(F32)

    pltpu.make_async_copy(got_parts, got_parts, p_recv.at[0]).wait()
    total = got_parts[:, 0] + got_parts[:, 1]
    total = total.reshape(experts * rows, 2, length)
    mean = total[:, 0, :]
    quad = total[:, 1, :]
    variance = NOISE + jnp.maximum(SIGNAL - quad, 0.0)
    gap = 0.5 * (jnp.log(jnp.full_like(variance, SIGNAL + NOISE)) - jnp.log(variance))
    weight = gap / variance
    weighted = weight * mean
    for j in range(blocks):
        on = taken_by[j] > 0.5
        sums_ref[j:j + 1, :] = jnp.sum(jnp.where(on, weighted, 0.0), axis=0, keepdims=True)
        sums_ref[blocks + j:blocks + j + 1, :] = jnp.sum(
            jnp.where(on, weight, 0.0), axis=0, keepdims=True)
    x_copy.wait_send()
    y_copy.wait_send()
    for copy in test_copies:
        copy.wait_send()
    for s in range(rows):
        sent = cols - 1 if order[s] is None else cols
        flat = sent_bytes.at[pl.ds(0, sent)]
        pltpu.make_async_copy(flat, flat, p_send.at[s]).wait()


def on_device(rows, cols, train_points, targets, inverse_factor, counts, membership, test_points):
    features, half = train_points.shape[1:]
    blocks, _, length = test_points.shape
    points = inverse_factor.shape[2]
    experts = cols // 2
    vmem, dma = pltpu.VMEM, pltpu.SemaphoreType.DMA
    anywhere = pl.BlockSpec(memory_space=pltpu.HBM)
    sums = pl.pallas_call(
        functools.partial(expert_kernel, rows, cols),
        out_shape=jax.ShapeDtypeStruct((2 * blocks, length), F32),
        in_specs=[anywhere] * 6,
        out_specs=pl.BlockSpec(memory_space=pltpu.VMEM),
        scratch_shapes=[
            vmem((half, points), F32),
            vmem((features, half), F32),
            vmem((1, half), F32),
            vmem((blocks, features, length), F32),
            vmem((features, half), F32),
            vmem((1, half), F32),
            vmem((rows - 1, features, length), F32),
            vmem((rows - 1, features, length), F32),
            vmem((half, points), BF16),
            vmem((half, points), BF16),
            vmem((points, 128), F32),
            vmem((points, 128), F32),
            vmem((points, 256), BF16),
            vmem((points, 2 * length), BF16),
            vmem((points, 2 * length), BF16),
            vmem((rows, 2, length), F32),
            vmem((experts, 2, rows, 2, length), F32),
            vmem((blocks, experts * rows, length), F32),
            vmem((cols, 2, length), F32),
            vmem((points, 128), F32),
            pltpu.SMEM(counts.shape, jnp.int32),
            pltpu.SMEM(membership.shape, jnp.int32),
            dma((6,)),
            dma((2,)),
            dma((2,)),
            dma((rows - 1,)),
            dma((rows - 1,)),
            dma((rows,)),
            dma((1,)),
        ],
        compiler_params=pltpu.CompilerParams(
            collective_id=0, has_side_effects=True
        ),
    )(counts, membership, train_points, targets, inverse_factor, test_points)
    precision_sum = 1.0 / (SIGNAL + NOISE) + sums[blocks:]
    return (sums[:blocks] / precision_sum, 1.0 / precision_sum)


def solution(mesh):
    in_specs = (
        P("row", None, "col"),
        P("row", "col"),
        P("row", "col", None),
        P("row", None),
        P(),
        P("row", None, None),
    )
    out_specs = (P("row", None), P("row", None))
    body = functools.partial(on_device, mesh.shape["row"], mesh.shape["col"])
    return jax.shard_map(
        body, mesh=mesh, in_specs=in_specs, out_specs=out_specs, check_vma=False
    )
```

time: 70.8 us -> 19.8 us (0.28)
  blocking collectives: 27.8 us -> 0 us
  Pallas kernels: 0 us -> 17.5 us
  local copies, waits for them, and re-layouts: 13.8 us -> 0 us
  matrix products: 9.53 us -> 0 us
  waiting for transfers between devices: 5.86 us -> 0 us
  starting transfers between devices: 5.72 us -> 0 us
  other arithmetic: 6.76 us -> 1.34 us
    pallas_call x0 -> x1, Pallas kernels: none -> 17.5 us  [on_device(): pl.pallas_call(functools.partial(expert_kernel, rows, cols), out_shape=ja...]
    all_gather x1 -> x0, blocking collectives: 15.2 us -> none  [on_device(): gathered = lax.all_gather(test_points, 'row', axis=0, tiled=True)]
    psum x1 -> x0, blocking collectives: 12.6 us -> none  [on_device(): total_num, total_wgt = lax.psum((placed[0], placed[1]), 'col')]
    dot_general x10 -> x0, matrix products: 9.53 us -> none  [the longest x2 2.25 us: cross_kernel(): products = jnp.einsum('dn,dp->np', train_cols, test_cols, precision=HIGHEST)]
    dynamic_slice x5 -> x0, local copies, waits for them, and re-layouts: 7.56 us -> none  [the longest x2 5.15 us: on_device(): lax.dynamic_index_in_dim(factor_pairs, 1 - parity, 2, keepdims=False)]
    all_to_all x1 -> x0, starting transfers between devices: 5.16 us -> none  [on_device(): lax.all_to_all(outgoing_sums, 'row', split_axis=0, concat_axis=0, tiled=T...]
    all_to_all x1 -> x0, waiting for transfers between devices: 4.81 us -> none  [on_device(): lax.all_to_all(outgoing_sums, 'row', split_axis=0, concat_axis=0, tiled=T...]
    unnamed x9 -> x0, local copies, waits for them, and re-layouts: 2.98 us -> none
  transfers between devices with their start and end apart: 3 -> 0, of which waited for: 2 -> 0; matrix products, arithmetic and copies ran while one was open for 32% -> 0% of each run, Pallas kernels for 0% -> 0%
where the time goes in v1:
time: 19.8 us; the launch traced here: 19.5 us
  Pallas kernels  17.5 us (88%)
  other arithmetic  1.34 us (7%)
  between operations  0.64 us (3%)
    pallas_call x1, Pallas kernels, on_device(): pl.pallas_call(functools.partial(expert_kernel, rows, cols), out_shape=ja...  17.5 us
    div x1, other arithmetic, on_device(): return (sums[:blocks] / precision_sum, 1.0 / precision_sum)  1.34 us

profile of v1, /device:TPU:0, one launch (start us, length us, event | category | flops | bytes accessed | tf_op | source)
XLA Modules:
  0.0 19.5 jit_solution(16294942082509077467)
XLA Ops:
  0.6 17.5 %shard_map.77 = f32[8,128]{1,0:T(8,128)} custom-call(s32[1,4]{1,0:T(1,128)} %counts_hbm.1, s32[4,4,16]{2,1,0:T(4,128)} %member_hbm.1, f32[1,32,512]{2,1,0:T(8,128)} %train_ref.1, f32[1,512]{1,0:T(1,128)} %target_ref.1, f32[1,512,1024]{2,1,0:T(8,128)} %factor_ref.1, f32[4,32,128]{2,1,0:T(8,128)} %test_ref.1), custom_call_target="tpu_custom_call" | custom-call | tf_op jit(solution)/shard_map/pallas_call | solution.py:242
  18.2 1.3 %fusion = (f32[4,128]{1,0:T(4,128)}, f32[4,128]{1,0:T(4,128)}) fusion(f32[8,128]{1,0:T(8,128)} %shard_map.77), kind=kLoop, calls=%fused_computation.2 | loop fusion | flops 1536 | bytes 8192 | tf_op jit(solution)/shard_map/div | solution.py:283

commit v2 on v1

--- a/solution.py
+++ b/solution.py
@@ -156,9 +156,11 @@
     chunk = 128
     order = [None] + list(range(rows - 1))
     owners = [row] + [lax.rem(row + rows - d - 1, rows) for d in range(rows - 1)]
-    for first in range(0, rows, 2):
+    groups = [(0,)] + [tuple(range(s, min(s + 2, rows))) for s in range(1, rows, 2)]
+    for group in groups:
+        wide = len(group) * length
         taken = []
-        for s in (first, first + 1):
+        for s in group:
             d = order[s]
             if d is None:
                 taken.append(tests[chosen_in(row, row)])
@@ -168,23 +170,23 @@
         t = jnp.concatenate(taken, axis=1)
         th, tl = high_low(2.0 * t)
         t2 = jnp.sum(t * t, axis=0, keepdims=True)
-        rhs = jnp.concatenate([th, th, tl, tl, tail_t], axis=0)
-        mean = jnp.zeros((1, pair), F32)
+        rhs = jnp.concatenate([th, th, tl, tl, tail_t[:, :wide]], axis=0)
+        mean = jnp.zeros((1, wide), F32)
         for i in range(0, 2 * half, chunk):
             e = jnp.dot(points[i:i + chunk, :], rhs, preferred_element_type=F32) - t2
             k = jnp.exp(e * (1.0 / features))
-            at = lax.broadcasted_iota(jnp.int32, (chunk, pair), 0) + i
+            at = lax.broadcasted_iota(jnp.int32, (chunk, wide), 0) + i
             k = jnp.where(at < valid, SIGNAL * k, 0.0)
             along = alpha[i:i + chunk, :]
-            mean += jnp.sum(k * jnp.concatenate([along, along], axis=1), axis=0, keepdims=True)
+            mean += jnp.sum(k * jnp.concatenate([along] * len(group), axis=1), axis=0, keepdims=True)
             kh, kl = high_low(k)
-            k_high[i:i + chunk, :] = kh
-            k_low[i:i + chunk, :] = kl
-        solved = jnp.dot(factor_high[...], k_high[...], preferred_element_type=F32)
-        solved += jnp.dot(factor_low[...], k_high[...], preferred_element_type=F32)
-        solved += jnp.dot(factor_high[...], k_low[...], preferred_element_type=F32)
+            k_high[i:i + chunk, :wide] = kh
+            k_low[i:i + chunk, :wide] = kl
+        solved = jnp.dot(factor_high[...], k_high[:, :wide], preferred_element_type=F32)
+        solved += jnp.dot(factor_low[...], k_high[:, :wide], preferred_element_type=F32)
+        solved += jnp.dot(factor_high[...], k_low[:, :wide], preferred_element_type=F32)
         quad = jnp.sum(solved * solved, axis=0, keepdims=True)
-        for n, s in enumerate((first, first + 1)):
+        for n, s in enumerate(group):
             lanes = slice(n * length, (n + 1) * length)
             d = order[s]
             sent_parts[s, 0:1, :] = mean[:, lanes]

time: 19.8 us -> 21.6 us (1.091)
  Pallas kernels: 17.5 us -> 19.3 us
    pallas_call x1, Pallas kernels: 17.5 us -> 19.3 us  [on_device(): pl.pallas_call(functools.partial(expert_kernel, rows, cols), out_shape=ja...]
where the time goes in v2:
time: 21.6 us; the launch traced here: 21.3 us
  Pallas kernels  19.3 us (89%)
  other arithmetic  1.34 us (6%)
  between operations  0.64 us (3%)
    pallas_call x1, Pallas kernels, on_device(): pl.pallas_call(functools.partial(expert_kernel, rows, cols), out_shape=ja...  19.3 us
    div x1, other arithmetic, on_device(): return (sums[:blocks] / precision_sum, 1.0 / precision_sum)  1.34 us

profile of v2, /device:TPU:0, one launch (start us, length us, event | category | flops | bytes accessed | tf_op | source)
XLA Modules:
  0.0 21.3 jit_solution(3497454781729127956)
XLA Ops:
  0.6 19.3 %shard_map.77 = f32[8,128]{1,0:T(8,128)} custom-call(s32[1,4]{1,0:T(1,128)} %counts_hbm.1, s32[4,4,16]{2,1,0:T(4,128)} %member_hbm.1, f32[1,32,512]{2,1,0:T(8,128)} %train_ref.1, f32[1,512]{1,0:T(1,128)} %target_ref.1, f32[1,512,1024]{2,1,0:T(8,128)} %factor_ref.1, f32[4,32,128]{2,1,0:T(8,128)} %test_ref.1), custom_call_target="tpu_custom_call" | custom-call | tf_op jit(solution)/shard_map/pallas_call | solution.py:244
  20.0 1.3 %fusion = (f32[4,128]{1,0:T(4,128)}, f32[4,128]{1,0:T(4,128)}) fusion(f32[8,128]{1,0:T(8,128)} %shard_map.77), kind=kLoop, calls=%fused_computation.2 | loop fusion | flops 1536 | bytes 8192 | tf_op jit(solution)/shard_map/div | solution.py:285
